TPU v7x, 256 devices: a whole 4x4x8 slice. The times are simulated.
256 devices in a mesh: spin: 2 (over core), band: 16 (over x, z_hi), grid: 8 (over z_lo, y).
Axes of the slice: x: 4, y: 4, z: 8 (z_hi: 4, z_lo: 2; z = z_hi * 2 + z_lo), core: 2. Of those that a mesh axis runs over, the one named last changes fastest.
Arguments:
- orbitals: bfloat16 [2, 128, 128, 128, 128], P('spin', 'band', 'grid'), may hold values from -0.14941406 to 0.14941406
- partial_bands: int32 [2, 2], P('spin'), may hold values from 0 to 127
- core_density: float32 [128, 128, 128], P('grid'), may hold values from 0.002 to 0.2
Outputs:
- potential: float32 [2, 128, 128, 128], P('spin', 'grid', 'band')
Inputs may be any that keep to these rules, and one draw needn't show every extreme that they name: `partial_bands`: row s holds, for spin s, the first half-occupied band and the count of half-occupied bands; bands past 128 - 1 do not exist.
All inputs are finite; a program needn't handle non-finite values.
Results may differ from a plain program's by a relative error of at most 0.0003.
Values sent between devices are 32-bit elements; how exact they have to be, the bound alone decides.
A program may use at most 128 MiB of HBM per device.

v0:
```python
import math

import jax
import jax.numpy as jnp
from jax import lax
from jax.experimental import pallas as pl
from jax.experimental.pallas import tpu as pltpu
from jax.sharding import PartitionSpec as P

KAPPA = 0.804
MU_X = 0.2195149727645171
BETA = 0.06672455060314922
GAMMA = (1.0 - math.log(2.0)) / math.pi**2
FZ_NORM = 2.0 ** (4.0 / 3.0) - 2.0
FPP_ZERO = 1.709921

MESH = pl.DeviceIdType.MESH
F32 = jnp.float32
N = 128
XR = 16
NX4 = 4
NZ4 = 4
GY = 4
GRID = 2 * GY
BAND = NX4 * NZ4
YB = N // BAND
YQ = N // NX4
CH = 3
HOPS = 5


def derivative_matrix():
    k = lax.broadcasted_iota(jnp.int32, (N, N), 0) - lax.broadcasted_iota(jnp.int32, (N, N), 1)
    far = jnp.abs(k)
    near = jnp.minimum(far, N - far)
    angle = (math.pi / N) * jnp.maximum(near, 1).astype(F32)
    size = (math.pi / N) * jnp.cos(angle) / jnp.sin(angle)
    flips = (k < 0).astype(jnp.int32) + (far > N // 2).astype(jnp.int32) + (far & 1)
    signed = jnp.where((flips & 1) == 1, -size, size)
    return jnp.where(k == 0, 0.0, signed)


def pw_fit(r, root, amp, alpha, b1, b2, b3, b4):
    denom = (2.0 * amp) * (root * (b1 + root * (b2 + root * (b3 + root * b4))))
    slope = (2.0 * amp) * (0.5 * b1 / root + (b2 + root * (1.5 * b3 + root * (2.0 * b4))))
    log = jnp.log(1.0 + 1.0 / denom)
    front = (-2.0 * amp) * (1.0 + alpha * r)
    value = front * log
    deriv = (-2.0 * amp * alpha) * log - front * slope / (denom * (denom + 1.0))
    return value, deriv


def cbrt(x):
    return jnp.exp(jnp.log(x) * (1.0 / 3.0))


def xc_derivs(own, other, s_own, s_mix, s_other):
    total = own + other
    inv_n = 1.0 / total
    c_own = cbrt(own)
    c_other = cbrt(other)
    c_tot = cbrt(total)
    inv_c = 1.0 / c_tot
    double = 2.0 * own
    kf = (6.0 * math.pi**2) ** (1.0 / 3.0) * c_own
    inv_kn = 1.0 / (kf * double)
    s2 = s_own * inv_kn * inv_kn
    inv_den = 1.0 / (1.0 + (MU_X / KAPPA) * s2)
    enh = (1.0 + KAPPA) - KAPPA * inv_den
    enh_d = MU_X * inv_den * inv_den
    dn_x = (-1.0 / math.pi) * kf * (enh - 2.0 * s2 * enh_d)
    ds_x = (-3.0 / (8.0 * math.pi)) * enh_d * inv_kn
    two13 = 2.0 ** (1.0 / 3.0)
    plus = double * inv_n
    minus = 2.0 * other * inv_n
    zeta = (own - other) * inv_n
    plus13 = two13 * c_own * inv_c
    minus13 = two13 * c_other * inv_c
    radius = (3.0 / (4.0 * math.pi)) ** (1.0 / 3.0) * inv_c
    root = jnp.sqrt(radius)
    ec0, ec0_r = pw_fit(radius, root, 0.031091, 0.2137, 7.5957, 3.5876, 1.6382, 0.49294)
    ec1, ec1_r = pw_fit(radius, root, 0.015545, 0.20548, 14.1189, 6.1977, 3.3662, 0.62517)
    ac, ac_r = pw_fit(radius, root, 0.016887, 0.11125, 10.357, 3.6231, 0.88026, 0.49671)
    fz = (plus * plus13 + minus * minus13 - 2.0) * (1.0 / FZ_NORM)
    fz_d = (4.0 / 3.0 / FZ_NORM) * (plus13 - minus13)
    z2 = zeta * zeta
    z3 = z2 * zeta
    z4 = z2 * z2
    w1 = (-1.0 / FPP_ZERO) * (1.0 - z4)
    diff = ec1 - ec0
    mix = ac * w1 + diff * z4
    ec = ec0 + fz * mix
    ec_r = ec0_r + fz * (ac_r * w1 + (ec1_r - ec0_r) * z4)
    ec_z = fz_d * mix + 4.0 * z3 * fz * (ac * (1.0 / FPP_ZERO) + diff)
    phi = 0.5 * (plus13 * plus13 + minus13 * minus13)
    phi_d = (1.0 / 3.0) * (1.0 / plus13 - 1.0 / minus13)
    inv_phi = 1.0 / phi
    phi3 = phi * phi * phi
    kf_tot = (3.0 * math.pi**2) ** (1.0 / 3.0)
    tfac = (math.pi / (16.0 * kf_tot)) * inv_phi * inv_phi * inv_c * inv_n * inv_n
    sigma = s_own + 2.0 * s_mix + s_other
    t2 = sigma * tfac
    inv_gp3 = (1.0 / GAMMA) * inv_phi * inv_phi * inv_phi
    ex = jnp.exp(-ec * inv_gp3)
    amp = (BETA / GAMMA) / (ex - 1.0)
    y = amp * t2
    den = 1.0 + y + y * y
    inv_d = 1.0 / den
    ct = (BETA / GAMMA) * t2
    q = ct * (1.0 + y) * inv_d
    grad_h = GAMMA * phi3 * jnp.log(1.0 + q)
    scale = GAMMA * phi3 / (1.0 + q) * inv_d * inv_d
    h_t = scale * ((BETA / GAMMA) * (1.0 + 2.0 * y))
    h_a = -scale * (ct * t2) * (y * (2.0 + y))
    h_ec = h_a * (amp * amp * ex * (GAMMA / BETA) * inv_gp3)
    h_phi = inv_phi * (3.0 * (grad_h - ec * h_ec) - 2.0 * t2 * h_t)
    one_ec = 1.0 + h_ec
    e_n = ec + grad_h - (1.0 / 3.0) * radius * ec_r * one_ec - (7.0 / 3.0) * t2 * h_t
    e_z = ec_z * one_ec + phi_d * h_phi
    dn = dn_x + e_n + e_z * minus
    ds_c = total * h_t * tfac
    return dn, ds_x + ds_c, 2.0 * ds_c


def kernel(
    orb_hbm, bands_hbm, core_hbm, out_ref,
    orb, dmat_ref, bands_ref, part, core, x_in, x_out, summed, z_in, zf_in, zf_sum, xf_in,
    dens, grad, grad_o, flux, turned, x_line, x_res, x_back, y_line, y_res, y_back, base, final, x_fin, y_fin,
    orb_sem, core_sem, bands_sem, hop_sem, xs_sem, xr_sem, zs_sem, zr_sem, fs_sem, fr_sem,
    ps_sem, pr_sem, ys_sem, yr_sem, gs_sem, gr_sem, bs_sem, br_sem,
):
    spin = lax.axis_index("spin")
    band = lax.axis_index("band")
    grid = lax.axis_index("grid")
    bx, bz = band // NZ4, lax.rem(band, NZ4)
    gz, gy = grid // GY, lax.rem(grid, GY)

    def half_of(z):
        q = z // 2
        return 3 * q + z * (1 - 2 * q)

    q, h, e = bz // 2, half_of(bz), lax.rem(bz, 2)
    member = 2 * bx + q
    partner = (1 - spin, band, grid)

    def at_band(x, z, core=spin):
        return (core, lax.rem(x, NX4) * NZ4 + lax.rem(z, NZ4), grid)

    def copy(src, dst, send_sem, recv_sem, device):
        return pltpu.make_async_remote_copy(
            src_ref=src, dst_ref=dst, send_sem=send_sem, recv_sem=recv_sem,
            device_id=device, device_id_type=MESH,
        )

    def send(*args):
        copy(*args).start()

    def sent(like, send_sem):
        copy(like, like, send_sem, send_sem, (spin, band, grid)).wait_send()

    def arrived(like, recv_sem):
        copy(like, like, recv_sem, recv_sem, (spin, band, grid)).wait_recv()

    def rows_at(start, count):
        return pl.ds(pl.multiple_of(start, 8), count)

    bands_copy = pltpu.make_async_copy(bands_hbm, bands_ref, bands_sem)
    bands_copy.start()
    z_all = 2 * bz + gz
    near = [at_band(bx + 1, bz), at_band(bx + 3, bz)]
    near += [(spin, band, gz * GY + lax.rem(gy + d, GY)) for d in (1, 3)]
    for d in (1, 7):
        z = lax.rem(z_all + d, 8)
        near += [(spin, bx * NZ4 + z // 2, lax.rem(z, 2) * GY + gy)]
    barrier = pltpu.get_barrier_semaphore()
    across = [(1 - spin, *peer[1:]) for peer in near]
    for peer in (*near, *across, partner):
        pl.semaphore_signal(barrier, inc=1, device_id=peer, device_id_type=MESH)

    def y_of(r):
        return pl.multiple_of(lax.rem(bx + r, NX4) * YQ, YQ)

    def y_at(r):
        return pl.ds(r * YQ, YQ)

    def load(k, cs, r):
        for c in cs:
            for half in range(2):
                pltpu.make_async_copy(
                    orb_hbm.at[0, :, pl.ds(8 * half + 2 * c, 2), pl.ds(y_of(r), YQ), :],
                    orb.at[:, c, half, :, y_at(r), :],
                    orb_sem.at[k],
                ).start()

    def loaded(k, window):
        pltpu.make_async_copy(window, window, orb_sem.at[k]).wait()

    load(0, (0,), 2)
    load(1, (1, 2), 2)
    for r in range(NX4):
        load(2, (3,), r)
    for k, r in ((3, 1), (4, 3), (5, 0)):
        load(k, (0, 1, 2), r)
    core_copy = pltpu.make_async_copy(
        core_hbm.at[rows_at(8 * h, 8), rows_at(YQ * bx + 16 * q, 16), :], core, core_sem
    )
    core_copy.start()

    with jax.named_scope("first_piece"):
        bands_copy.wait()
        first = bands_ref[0, 0]
        last = first + bands_ref[0, 1]
        weights = []
        for b in range(8):
            ident = band * 8 + b
            weights.append(jnp.where((ident >= first) & (ident < last), 0.5, 1.0).astype(F32))

    def density(c, r):
        acc = None
        for b in range(8):
            v = orb[b, c, :, :, r * YQ : (r + 1) * YQ, :].astype(F32)
            term = weights[b] * (v * v)
            acc = term if acc is None else acc + term
        part[r, c] = acc

    plus, minus = at_band(bx + 1, bz), at_band(bx + 3, bz)

    def x_send(stream, c, src):
        target = minus if stream % 2 else plus
        send(src, x_in.at[c, stream], xs_sem, xr_sem.at[c, int(stream > 1)], target)

    def far(c):
        x_send(0, c, part.at[2, c, 0])
        x_send(1, c, part.at[2, c, 1])

    def direct(c):
        x_send(2, c, part.at[1, c, 1])
        x_send(3, c, part.at[3, c, 0])

    def relay(c):
        arrived(x_in.at[c, 0:2], xr_sem.at[c, 0])
        for side, r in ((0, 1), (1, 3)):
            x_out[side, c] = part[r, c, side] + x_in[c, side]
            x_send(4 + side, c, x_out.at[side, c])

    def z_targets(ds, core):
        for d in ds:
            z = lax.rem(bz + d, NZ4)
            yield d, half_of(z), rows_at(16 * (z // 2), 16), at_band(bx, z, core)

    def finish(c):
        arrived(x_in.at[c, 2:6], xr_sem.at[c, 1])
        summed[c, 0] = part[0, c, 0] + x_in[c, 4] + x_in[c, 3]
        summed[c, 1] = part[0, c, 1] + x_in[c, 5] + x_in[c, 2]
        for slot, half, ys, device in z_targets((2, 1, 3, 0), 1 - spin):
            send(summed.at[c, half, :, ys, :], z_in.at[slot, c], zs_sem, zr_sem, device)

    def z_first(ds):
        for slot, half, ys, device in z_targets(ds, spin):
            send(part.at[:, 3, half, :, ys, :], zf_in.at[slot - 1], fs_sem.at[0], fr_sem.at[0], device)

    def tell(k):
        for peer in near:
            pl.semaphore_signal(hop_sem.at[k - 1], inc=1, device_id=peer, device_id_type=MESH)

    def hear(k):
        pl.semaphore_wait(hop_sem.at[k - 1], len(near))
        if k < HOPS:
            tell(k + 1)

    loaded(0, orb.at[:, 0, :, :, y_at(2), :])
    density(0, 2)
    with jax.named_scope("barrier"):
        pl.semaphore_wait(barrier, 2 * len(near) + 1)
    with jax.named_scope("rs_head"):
        far(0)
        tell(1)
        loaded(1, orb.at[:, 1:3, :, :, y_at(2), :])
        density(1, 2)
        far(1)
        density(2, 2)
        far(2)
        loaded(2, orb.at[:, 3])
        for r in range(NX4):
            density(3, r)
        loaded(3, orb.at[:, 0:3, :, :, y_at(1), :])
        loaded(4, orb.at[:, 0:3, :, :, y_at(3), :])
        density(0, 1)
        density(0, 3)
        direct(0)
    with jax.named_scope("hear1"):
        hear(1)
        for d in (1, 3):
            pl.semaphore_signal(
                hop_sem.at[HOPS], inc=1, device_id=at_band(bx, bz + d), device_id_type=MESH
            )
        z_first((1, 3))
    with jax.named_scope("rs_rest"):
        loaded(5, orb.at[:, 0:3, :, :, y_at(0), :])
        for c, r in ((1, 1), (1, 3), (2, 1), (2, 3), (0, 0), (1, 0), (2, 0)):
            density(c, r)
        dmat_ref[...] = derivative_matrix()
    with jax.named_scope("hear_z"):
        pl.semaphore_wait(hop_sem.at[HOPS], 2)
        z_first((2,))
    for c in range(CH):
        with jax.named_scope(f"relay{c}"):
            relay(c)
        if c + 1 < CH:
            direct(c + 1)
    core_copy.wait()
    with jax.named_scope("hear2"):
        hear(2)
    with jax.named_scope("finish0"):
        finish(0)
    with jax.named_scope("hear3"):
        hear(3)
    for c in range(1, CH):
        with jax.named_scope(f"finish{c}"):
            finish(c)

    y_mine = rows_at(16 * q, 16)
    with jax.named_scope("zf_wait"):
        arrived(zf_in, fr_sem.at[0])
        zf_sum[...] = part[:, 3, h, :, y_mine, :] + zf_in[0] + zf_in[1] + zf_in[2]
        for r in (2, 1, 3, 0):
            send(
                zf_sum.at[r], xf_in.at[r], fs_sem.at[1], fr_sem.at[1],
                at_band(bx + r, bz, 1 - spin),
            )
    with jax.named_scope("hear4"):
        hear(4)
    with jax.named_scope("z_wait"):
        arrived(z_in, zr_sem)
    for c in range(CH):
        block = 0.5 * core[2 * c : 2 * c + 2] + z_in[0, c] + z_in[1, c] + z_in[2, c] + z_in[3, c]
        dens[32 * c : 32 * c + 32, :] = block.reshape(32, N)
    with jax.named_scope("hear5"):
        hear(5)
    with jax.named_scope("xf_wait"):
        arrived(xf_in, fr_sem.at[1])
    block = 0.5 * core[2 * CH : 2 * CH + 2] + xf_in[0] + xf_in[1] + xf_in[2] + xf_in[3]
    dens[32 * CH : 32 * CH + 32, :] = block.reshape(32, N)

    def dot(a, b):
        return jnp.dot(a, b, precision=lax.Precision.HIGHEST, preferred_element_type=F32)

    holder = 1 - spin

    def y_exchange(src, dst, k):
        for dx, dq in ((2, 1), (1, 1), (3, 1), (0, 1), (2, 0), (1, 0), (3, 0)):
            x, place = lax.rem(bx + dx, NX4), lax.rem(q + dq, 2)
            z = h + place * (3 - 2 * h)
            send(
                src.at[rows_at(16 * (2 * x + place), 16), :], dst.at[rows_at(16 * member, 16), :],
                ys_sem.at[k], yr_sem.at[k], (holder, x * NZ4 + z, grid),
            )
        mine = rows_at(16 * member, 16)
        send(src.at[mine, :], dst.at[mine, :], ys_sem.at[k], yr_sem.at[k], partner)

    def y_wait(dst, k):
        arrived(dst, yr_sem.at[k])

    def x_exchange(src, dst, k):
        for de in (1, 0):
            for dz in (1, 0):
                for dy in (2, 1, 3, 0):
                    if (de, dz, dy) == (0, 0, 0):
                        continue
                    e2 = lax.rem(e + de, 2)
                    g2 = lax.rem(gz + dz, 2) * GY + lax.rem(gy + dy, GY)
                    z = 2 * q + e2
                    there, here = 8 * e2 + g2, 2 * grid + h
                    if k == 1:
                        there, here = 2 * g2 + half_of(z), 8 * e + grid
                    send(
                        src.at[rows_at(8 * there, 8), :], dst.at[rows_at(8 * here, 8), :],
                        gs_sem.at[k], gr_sem.at[k], (holder, bx * NZ4 + z, g2),
                    )
        mine = (2 * grid + h, 8 * e + grid)
        there, here = mine if k == 1 else mine[::-1]
        there, here = rows_at(8 * there, 8), rows_at(8 * here, 8)
        send(src.at[there, :], dst.at[here, :], gs_sem.at[k], gr_sem.at[k], partner)

    def x_wait(dst, k):
        arrived(dst, gr_sem.at[k])

    def out_y():
        xr = 8 * h + member
        for dx in (2, 1, 3, 0):
            for dz in (2, 1, 3, 0):
                b2 = lax.rem(bx + dx, NX4) * NZ4 + lax.rem(bz + dz, NZ4)
                send(
                    y_res.at[1, rows_at(8 * b2, 8), :], y_fin.at[rows_at(8 * xr, 8), :],
                    ys_sem.at[3], yr_sem.at[3], (holder, b2, grid),
                )

    def out_x():
        for dz, dy in ((1, 2), (1, 1), (1, 3), (0, 2), (1, 0), (0, 1), (0, 3), (0, 0)):
            g2 = lax.rem(gz + dz, 2) * GY + lax.rem(gy + dy, GY)
            send(
                x_res.at[1, rows_at(XR * g2, XR), :], x_fin.at[rows_at(XR * grid, XR), :],
                gs_sem.at[3], gr_sem.at[3], (holder, band, g2),
            )

    def pencils(y_src, x_src, k):
        y_exchange(y_src, y_line.at[k], 2 * k)
        for t in range(16):
            turned[k, 8 * t : 8 * t + 8, :] = x_src[pl.ds(t, 8, stride=16), :]
        x_exchange(turned.at[k], x_line.at[k], 2 * k)

    dmat = dmat_ref[...]

    with jax.named_scope("fwd0"):
        pencils(dens, dens, 0)
        send(dens, grad_o.at[3], ps_sem, pr_sem, partner)
        grad[2] = -dot(dens[...], dmat)
        send(grad.at[2], grad_o.at[2], ps_sem, pr_sem, partner)
    with jax.named_scope("drain0"):
        sent(part.at[0:3, 0:CH], xs_sem)
        sent(z_in, zs_sem)
        sent(zf_in, fs_sem.at[0])
        sent(xf_in, fs_sem.at[1])
    with jax.named_scope("y_wait0"):
        y_wait(y_line.at[0], 0)
    with jax.named_scope("y_lines0"):
        y_res[0] = dot(dmat, y_line[0])
        y_exchange(y_res.at[0], y_back, 1)
    with jax.named_scope("x_wait0"):
        x_wait(x_line.at[0], 0)
    with jax.named_scope("x_lines0"):
        x_res[0] = dot(dmat, x_line[0])
        x_exchange(x_res.at[0], x_back, 1)
    with jax.named_scope("y_back0"):
        y_wait(y_back, 1)
        send(y_back, grad_o.at[1], ps_sem, pr_sem, partner)
    with jax.named_scope("x_back0"):
        x_wait(x_back, 1)
        for i in range(8):
            grad[0, 16 * i : 16 * i + 16, :] = x_back[pl.ds(i, 16, stride=8), :]
    with jax.named_scope("swap"):
        send(grad.at[0], grad_o.at[0], ps_sem, pr_sem, partner)
        arrived(grad_o, pr_sem)

    with jax.named_scope("xc"):
        step = 16
        for i in range(0, N, step):
            rows = slice(i, i + step)
            o = (grad[0, rows, :], y_back[rows, :], grad[2, rows, :])
            g = (grad_o[0, rows, :], grad_o[1, rows, :], grad_o[2, rows, :])
            s_own = g[0] * g[0] + g[1] * g[1] + g[2] * g[2]
            s_mix = g[0] * o[0] + g[1] * o[1] + g[2] * o[2]
            s_other = o[0] * o[0] + o[1] * o[1] + o[2] * o[2]
            dn, ds, dm = xc_derivs(grad_o[3, rows, :], dens[rows, :], s_own, s_mix, s_other)
            for a in range(3):
                flux[a, rows, :] = 2.0 * ds * g[a] + dm * o[a]
            flux[3, rows, :] = dn

    with jax.named_scope("fwd1"):
        pencils(flux.at[1], flux.at[0], 1)
        base[...] = (flux[3] + dot(flux[2], dmat)).reshape(8, 16, N)
        there = lax.rem(e + 1, 2)
        send(
            base.at[:, rows_at(8 * there, 8), :], final.at[h],
            bs_sem, br_sem, (spin, bx * NZ4 + 2 * q + there, grid),
        )
        final[h] = base[:, rows_at(8 * e, 8), :]
    with jax.named_scope("drain1"):
        for k in (0, 1):
            sent(y_line.at[k], ys_sem.at[k])
            sent(x_line.at[k], gs_sem.at[k])
        sent(grad_o, ps_sem)
    with jax.named_scope("y_wait1"):
        y_wait(y_line.at[1], 2)
    with jax.named_scope("y_lines1"):
        y_res[1] = dot(dmat, y_line[1])
        out_y()
    with jax.named_scope("x_wait1"):
        x_wait(x_line.at[1], 2)
    with jax.named_scope("x_lines1"):
        x_res[1] = dot(dmat, x_line[1])
        out_x()
    with jax.named_scope("drain2"):
        for k in (2, 3):
            sent(y_line.at[0], ys_sem.at[k])
            sent(x_line.at[0], gs_sem.at[k])
        sent(final.at[0], bs_sem)
        arrived(final.at[0], br_sem)
    with jax.named_scope("x_back1"):
        arrived(x_fin, gr_sem.at[3])
        for i in range(XR):
            out_ref[0, i] = final[i // 8, i % 8] - x_fin[pl.ds(i, YB, stride=XR), :]
    with jax.named_scope("y_back1"):
        arrived(y_fin, yr_sem.at[3])
    with jax.named_scope("tail"):
        out_ref[0] = out_ref[0] - y_fin[...].reshape(XR, YB, N)


def per_device(orbitals, partial_bands, core_density):
    vm = pltpu.VMEM
    sem = pltpu.SemaphoreType.DMA
    anyspace = pl.BlockSpec(memory_space=pltpu.HBM)
    return pl.pallas_call(
        kernel,
        out_shape=jax.ShapeDtypeStruct((1, XR, YB, N), F32),
        in_specs=[anyspace] * 3,
        out_specs=pl.BlockSpec(memory_space=pltpu.VMEM),
        scratch_shapes=[
            vm((8, CH + 1, 2, 2, N, N), jnp.bfloat16),
            vm((N, N), F32),
            pltpu.SMEM((1, 2), jnp.int32),
            vm((NX4, CH + 1, 2, 2, YQ, N), F32),
            vm((8, 16, N), F32),
            vm((CH, 6, 2, YQ, N), F32),
            vm((2, CH, 2, YQ, N), F32),
            vm((CH, 2, 2, YQ, N), F32),
            vm((NZ4, CH, 2, 16, N), F32),
            vm((NZ4 - 1, NX4, 2, 16, N), F32),
            vm((NX4, 2, 16, N), F32),
            vm((NX4, 2, 16, N), F32),
            vm((N, N), F32),
            vm((3, N, N), F32),
            vm((4, N, N), F32),
            vm((4, N, N), F32),
            vm((2, N, N), F32),
            vm((2, N, N), F32),
            vm((2, N, N), F32),
            vm((N, N), F32),
            vm((2, N, N), F32),
            vm((2, N, N), F32),
            vm((N, N), F32),
            vm((8, 16, N), F32),
            vm((2, 8, YB, N), F32),
            vm((N, N), F32),
            vm((N, N), F32),
            sem((6,)),
            sem,
            sem,
            pltpu.SemaphoreType.REGULAR((HOPS + 1,)),
            sem,
            sem((CH, 2)),
            sem,
            sem,
            sem((2,)),
            sem((2,)),
            sem,
            sem,
            sem((4,)),
            sem((4,)),
            sem((4,)),
            sem((4,)),
            sem,
            sem,
        ],
        compiler_params=pltpu.CompilerParams(
            collective_id=0, has_side_effects=True, vmem_limit_bytes=54400 * 1024
        ),
    )(orbitals, partial_bands, core_density)


def solution(mesh):
    in_specs = (P("spin", "band", "grid", None, None), P("spin", None), P("grid", None, None))
    out_specs = P("spin", "grid", "band", None)

    return jax.shard_map(
        per_device, mesh=mesh, in_specs=in_specs, out_specs=out_specs, check_vma=False
    )
```

profile of v0, /device:TPU:1, one launch (start us, length us, event | category | flops | bytes accessed | tf_op | source)
XLA Modules:
  0.0 47.6 jit_solution(15352487314146267149)
XLA Ops:
  0.0 0.0 copy-start
  0.0 0.7 %copy-done = s32[1,2]{1,0:T(1,128)S(1)} copy-done((s32[1,2]{1,0:T(1,128)S(1)}, s32[1,2]{1,0:T(1,128)}, u32[]{:S(2)}) %copy-start) | copy-done | bytes 32
  0.7 46.3 %shard_map.37 = f32[1,16,8,128]{3,2,1,0:T(8,128)S(1)} custom-call(bf16[1,8,16,128,128]{4,3,2,1,0:T(8,128)(2,1)} %orb_hbm.1, s32[1,2]{1,0:T(1,128)S(1)} %copy-done, f32[16,128,128]{2,1,0:T(8,128)} %core_hbm.1), custom_call_target="tpu_custom_call" | custom-call | tf_op jit(solution)/shard_map/pallas_call | solution.py:503
  47.0 0.6 %copy.5 = f32[1,16,8,128]{3,2,1,0:T(8,128)} copy(f32[1,16,8,128]{3,2,1,0:T(8,128)S(1)} %shard_map.37) | data formatting | bytes 131072
Async XLA Ops:
  0.0 0.7 %copy-start = (s32[1,2]{1,0:T(1,128)S(1)}, s32[1,2]{1,0:T(1,128)}, u32[]{:S(2)}) copy-start(s32[1,2]{1,0:T(1,128)} %bands_hbm.1) | copy-start | bytes 28
where the time goes:
time: 47.7 us; the launch traced here: 47.6 us
  Pallas kernels  46.3 us (97%)
  local copies, waits for them, and re-layouts  1.29 us (3%)
    pallas_call x1, Pallas kernels, per_device(): pl.pallas_call(kernel, out_shape=jax.ShapeDtypeStruct((1, XR, YB, N), F32...  46.3 us
    unnamed x3, local copies, waits for them, and re-layouts  1.29 us

commit v1 on v0

--- a/solution.py
+++ b/solution.py
@@ -124,7 +124,7 @@
 
 def kernel(
     orb_hbm, bands_hbm, core_hbm, out_ref,
-    orb, dmat_ref, bands_ref, part, core, x_in, x_out, summed, z_in, zf_in, zf_sum, xf_in,
+    orb, dmat_ref, lane_ref, bands_ref, part, core, x_in, x_out, summed, z_in, zf_in, zf_sum, xf_in,
     dens, grad, grad_o, flux, turned, x_line, x_res, x_back, y_line, y_res, y_back, base, final, x_fin, y_fin,
     orb_sem, core_sem, bands_sem, hop_sem, xs_sem, xr_sem, zs_sem, zr_sem, fs_sem, fr_sem,
     ps_sem, pr_sem, ys_sem, yr_sem, gs_sem, gr_sem, bs_sem, br_sem,
@@ -174,7 +174,9 @@
         near += [(spin, bx * NZ4 + z // 2, lax.rem(z, 2) * GY + gy)]
     barrier = pltpu.get_barrier_semaphore()
     across = [(1 - spin, *peer[1:]) for peer in near]
-    for peer in (*near, *across, partner):
+    aside = [at_band(bx, bz + d) for d in (1, 3)]
+    entry = (*near, *across, partner, *aside)
+    for peer in entry:
         pl.semaphore_signal(barrier, inc=1, device_id=peer, device_id_type=MESH)
 
     def y_of(r):
@@ -196,9 +198,9 @@
         pltpu.make_async_copy(window, window, orb_sem.at[k]).wait()
 
     load(0, (0,), 2)
-    load(1, (1, 2), 2)
     for r in range(NX4):
         load(2, (3,), r)
+    load(1, (1, 2), 2)
     for k, r in ((3, 1), (4, 3), (5, 0)):
         load(k, (0, 1, 2), r)
     core_copy = pltpu.make_async_copy(
@@ -250,6 +252,8 @@
 
     def finish(c):
         arrived(x_in.at[c, 2:6], xr_sem.at[c, 1])
+        if c == 0:
+            hear(3)
         summed[c, 0] = part[0, c, 0] + x_in[c, 4] + x_in[c, 3]
         summed[c, 1] = part[0, c, 1] + x_in[c, 5] + x_in[c, 2]
         for slot, half, ys, device in z_targets((2, 1, 3, 0), 1 - spin):
@@ -259,6 +263,13 @@
         for slot, half, ys, device in z_targets(ds, spin):
             send(part.at[:, 3, half, :, ys, :], zf_in.at[slot - 1], fs_sem.at[0], fr_sem.at[0], device)
 
+    def dmat_table():
+        table = derivative_matrix()
+        hi = table.astype(jnp.bfloat16)
+        lo = (table - hi.astype(F32)).astype(jnp.bfloat16)
+        dmat_ref[...] = jnp.concatenate([hi, hi, lo], 1)
+        lane_ref[...] = jnp.concatenate([hi, lo, hi], 0)
+
     def tell(k):
         for peer in near:
             pl.semaphore_signal(hop_sem.at[k - 1], inc=1, device_id=peer, device_id_type=MESH)
@@ -271,38 +282,37 @@
     loaded(0, orb.at[:, 0, :, :, y_at(2), :])
     density(0, 2)
     with jax.named_scope("barrier"):
-        pl.semaphore_wait(barrier, 2 * len(near) + 1)
+        pl.semaphore_wait(barrier, len(entry))
     with jax.named_scope("rs_head"):
         far(0)
+        for peer in aside:
+            pl.semaphore_signal(hop_sem.at[HOPS], inc=1, device_id=peer, device_id_type=MESH)
         tell(1)
+        loaded(2, orb.at[:, 3])
+        for r in range(NX4):
+            density(3, r)
+        z_first((1, 3))
         loaded(1, orb.at[:, 1:3, :, :, y_at(2), :])
         density(1, 2)
         far(1)
         density(2, 2)
         far(2)
-        loaded(2, orb.at[:, 3])
-        for r in range(NX4):
-            density(3, r)
         loaded(3, orb.at[:, 0:3, :, :, y_at(1), :])
         loaded(4, orb.at[:, 0:3, :, :, y_at(3), :])
         density(0, 1)
         density(0, 3)
         direct(0)
-    with jax.named_scope("hear1"):
-        hear(1)
-        for d in (1, 3):
-            pl.semaphore_signal(
-                hop_sem.at[HOPS], inc=1, device_id=at_band(bx, bz + d), device_id_type=MESH
-            )
-        z_first((1, 3))
-    with jax.named_scope("rs_rest"):
-        loaded(5, orb.at[:, 0:3, :, :, y_at(0), :])
-        for c, r in ((1, 1), (1, 3), (2, 1), (2, 3), (0, 0), (1, 0), (2, 0)):
+        for c, r in ((1, 1), (1, 3), (2, 1), (2, 3)):
             density(c, r)
-        dmat_ref[...] = derivative_matrix()
     with jax.named_scope("hear_z"):
         pl.semaphore_wait(hop_sem.at[HOPS], 2)
         z_first((2,))
+    with jax.named_scope("rs_rest"):
+        hear(1)
+        loaded(5, orb.at[:, 0:3, :, :, y_at(0), :])
+        for c in range(CH):
+            density(c, 0)
+        dmat_table()
     for c in range(CH):
         with jax.named_scope(f"relay{c}"):
             relay(c)
@@ -311,11 +321,7 @@
     core_copy.wait()
     with jax.named_scope("hear2"):
         hear(2)
-    with jax.named_scope("finish0"):
-        finish(0)
-    with jax.named_scope("hear3"):
-        hear(3)
-    for c in range(1, CH):
+    for c in range(CH):
         with jax.named_scope(f"finish{c}"):
             finish(c)
 
@@ -342,8 +348,17 @@
     block = 0.5 * core[2 * CH : 2 * CH + 2] + xf_in[0] + xf_in[1] + xf_in[2] + xf_in[3]
     dens[32 * CH : 32 * CH + 32, :] = block.reshape(32, N)
 
-    def dot(a, b):
-        return jnp.dot(a, b, precision=lax.Precision.HIGHEST, preferred_element_type=F32)
+    def halves(x):
+        hi = x.astype(jnp.bfloat16)
+        return hi, (x - hi.astype(F32)).astype(jnp.bfloat16)
+
+    def along_rows(x):
+        hi, lo = halves(x)
+        return jnp.dot(dmat_ref[...], jnp.concatenate([hi, lo, hi], 0), preferred_element_type=F32)
+
+    def along_lanes(x):
+        hi, lo = halves(x)
+        return jnp.dot(jnp.concatenate([hi, hi, lo], 1), lane_ref[...], preferred_element_type=F32)
 
     holder = 1 - spin
 
@@ -409,12 +424,10 @@
             turned[k, 8 * t : 8 * t + 8, :] = x_src[pl.ds(t, 8, stride=16), :]
         x_exchange(turned.at[k], x_line.at[k], 2 * k)
 
-    dmat = dmat_ref[...]
-
     with jax.named_scope("fwd0"):
         pencils(dens, dens, 0)
         send(dens, grad_o.at[3], ps_sem, pr_sem, partner)
-        grad[2] = -dot(dens[...], dmat)
+        grad[2] = -along_lanes(dens[...])
         send(grad.at[2], grad_o.at[2], ps_sem, pr_sem, partner)
     with jax.named_scope("drain0"):
         sent(part.at[0:3, 0:CH], xs_sem)
@@ -424,12 +437,12 @@
     with jax.named_scope("y_wait0"):
         y_wait(y_line.at[0], 0)
     with jax.named_scope("y_lines0"):
-        y_res[0] = dot(dmat, y_line[0])
+        y_res[0] = along_rows(y_line[0])
         y_exchange(y_res.at[0], y_back, 1)
     with jax.named_scope("x_wait0"):
         x_wait(x_line.at[0], 0)
     with jax.named_scope("x_lines0"):
-        x_res[0] = dot(dmat, x_line[0])
+        x_res[0] = along_rows(x_line[0])
         x_exchange(x_res.at[0], x_back, 1)
     with jax.named_scope("y_back0"):
         y_wait(y_back, 1)
@@ -458,7 +471,7 @@
 
     with jax.named_scope("fwd1"):
         pencils(flux.at[1], flux.at[0], 1)
-        base[...] = (flux[3] + dot(flux[2], dmat)).reshape(8, 16, N)
+        base[...] = (flux[3] + along_lanes(flux[2])).reshape(8, 16, N)
         there = lax.rem(e + 1, 2)
         send(
             base.at[:, rows_at(8 * there, 8), :], final.at[h],
@@ -473,12 +486,12 @@
     with jax.named_scope("y_wait1"):
         y_wait(y_line.at[1], 2)
     with jax.named_scope("y_lines1"):
-        y_res[1] = dot(dmat, y_line[1])
+        y_res[1] = along_rows(y_line[1])
         out_y()
     with jax.named_scope("x_wait1"):
         x_wait(x_line.at[1], 2)
     with jax.named_scope("x_lines1"):
-        x_res[1] = dot(dmat, x_line[1])
+        x_res[1] = along_rows(x_line[1])
         out_x()
     with jax.named_scope("drain2"):
         for k in (2, 3):
@@ -507,7 +520,8 @@
         out_specs=pl.BlockSpec(memory_space=pltpu.VMEM),
         scratch_shapes=[
             vm((8, CH + 1, 2, 2, N, N), jnp.bfloat16),
-            vm((N, N), F32),
+            vm((N, 3 * N), jnp.bfloat16),
+            vm((3 * N, N), jnp.bfloat16),
             pltpu.SMEM((1, 2), jnp.int32),
             vm((NX4, CH + 1, 2, 2, YQ, N), F32),
             vm((8, 16, N), F32),

time: 47.7 us -> 45.8 us (0.960)
  Pallas kernels: 46.3 us -> 44.5 us
    pallas_call x1, Pallas kernels: 46.3 us -> 44.5 us  [per_device(): pl.pallas_call(kernel, out_shape=jax.ShapeDtypeStruct((1, XR, YB, N), F32...]
where the time goes in v1:
time: 45.8 us
  Pallas kernels  44.5 us (97%)
  local copies, waits for them, and re-layouts  1.29 us (3%)
    pallas_call x1, Pallas kernels, per_device(): pl.pallas_call(kernel, out_shape=jax.ShapeDtypeStruct((1, XR, YB, N), F32...  44.5 us
    unnamed x3, local copies, waits for them, and re-layouts  1.29 us

profile of v1, /device:TPU:1, one launch (start us, length us, event | category | flops | bytes accessed | tf_op | source)
XLA Modules:
  0.0 45.8 jit_solution(14129914512377591233)
XLA Ops:
  0.0 0.0 copy-start
  0.0 0.7 %copy-done = s32[1,2]{1,0:T(1,128)S(1)} copy-done((s32[1,2]{1,0:T(1,128)S(1)}, s32[1,2]{1,0:T(1,128)}, u32[]{:S(2)}) %copy-start) | copy-done | bytes 32
  0.7 44.5 %shard_map.37 = f32[1,16,8,128]{3,2,1,0:T(8,128)S(1)} custom-call(bf16[1,8,16,128,128]{4,3,2,1,0:T(8,128)(2,1)} %orb_hbm.1, s32[1,2]{1,0:T(1,128)S(1)} %copy-done, f32[16,128,128]{2,1,0:T(8,128)} %core_hbm.1), custom_call_target="tpu_custom_call" | custom-call | tf_op jit(solution)/shard_map/pallas_call | solution.py:516
  45.1 0.6 %copy.5 = f32[1,16,8,128]{3,2,1,0:T(8,128)} copy(f32[1,16,8,128]{3,2,1,0:T(8,128)S(1)} %shard_map.37) | data formatting | bytes 131072
Async XLA Ops:
  0.0 0.7 %copy-start = (s32[1,2]{1,0:T(1,128)S(1)}, s32[1,2]{1,0:T(1,128)}, u32[]{:S(2)}) copy-start(s32[1,2]{1,0:T(1,128)} %bands_hbm.1) | copy-start | bytes 28

commit v2 on v1

--- a/solution.py
+++ b/solution.py
@@ -569,7 +569,7 @@
         compiler_params=pltpu.CompilerParams(
             collective_id=0, has_side_effects=True, vmem_limit_bytes=54400 * 1024
         ),
-    )(orbitals, partial_bands, core_density)
+    )(*[pltpu.with_memory_space_constraint(a, pltpu.HBM) for a in (orbitals, partial_bands, core_density)])
 
 
 def solution(mesh):

time: 45.8 us -> 44.7 us (0.976)
  local copies, waits for them, and re-layouts: 1.29 us -> 0.63 us
  Pallas kernels: 44.5 us -> 44 us
    unnamed x3 -> x1, local copies, waits for them, and re-layouts: 1.29 us -> 0.63 us
where the time goes in v2:
time: 44.7 us
  Pallas kernels  44 us (98%)
  local copies, waits for them, and re-layouts  0.63 us (1%)
    pallas_call x1, Pallas kernels, per_device(): pl.pallas_call(kernel, out_shape=jax.ShapeDtypeStruct((1, XR, YB, N), F32...  44 us

profile of v2, /device:TPU:1, one launch (start us, length us, event | category | flops | bytes accessed | tf_op | source)
XLA Modules:
  0.0 44.7 jit_solution(9640801997624859212)
XLA Ops:
  0.0 44.0 %shard_map.37 = f32[1,16,8,128]{3,2,1,0:T(8,128)S(1)} custom-call(bf16[1,8,16,128,128]{4,3,2,1,0:T(8,128)(2,1)} %orb_hbm.1, s32[1,2]{1,0:T(1,128)} %bands_hbm.1, f32[16,128,128]{2,1,0:T(8,128)} %core_hbm.1), custom_call_target="tpu_custom_call" | custom-call | tf_op jit(solution)/shard_map/pallas_call | solution.py:516
  44.0 0.6 %copy.5 = f32[1,16,8,128]{3,2,1,0:T(8,128)} copy(f32[1,16,8,128]{3,2,1,0:T(8,128)S(1)} %shard_map.37) | data formatting | bytes 131072

commit v3 on v2

--- a/solution.py
+++ b/solution.py
@@ -54,7 +54,7 @@
     return jnp.exp(jnp.log(x) * (1.0 / 3.0))
 
 
-def xc_derivs(own, other, s_own, s_mix, s_other):
+def xc_prepare(own, other):
     total = own + other
     inv_n = 1.0 / total
     c_own = cbrt(own)
@@ -64,12 +64,6 @@
     double = 2.0 * own
     kf = (6.0 * math.pi**2) ** (1.0 / 3.0) * c_own
     inv_kn = 1.0 / (kf * double)
-    s2 = s_own * inv_kn * inv_kn
-    inv_den = 1.0 / (1.0 + (MU_X / KAPPA) * s2)
-    enh = (1.0 + KAPPA) - KAPPA * inv_den
-    enh_d = MU_X * inv_den * inv_den
-    dn_x = (-1.0 / math.pi) * kf * (enh - 2.0 * s2 * enh_d)
-    ds_x = (-3.0 / (8.0 * math.pi)) * enh_d * inv_kn
     two13 = 2.0 ** (1.0 / 3.0)
     plus = double * inv_n
     minus = 2.0 * other * inv_n
@@ -95,28 +89,43 @@
     phi = 0.5 * (plus13 * plus13 + minus13 * minus13)
     phi_d = (1.0 / 3.0) * (1.0 / plus13 - 1.0 / minus13)
     inv_phi = 1.0 / phi
-    phi3 = phi * phi * phi
+    gp3 = GAMMA * phi * phi * phi
     kf_tot = (3.0 * math.pi**2) ** (1.0 / 3.0)
     tfac = (math.pi / (16.0 * kf_tot)) * inv_phi * inv_phi * inv_c * inv_n * inv_n
-    sigma = s_own + 2.0 * s_mix + s_other
-    t2 = sigma * tfac
     inv_gp3 = (1.0 / GAMMA) * inv_phi * inv_phi * inv_phi
     ex = jnp.exp(-ec * inv_gp3)
     amp = (BETA / GAMMA) / (ex - 1.0)
+    amp_ec = amp * amp * ex * (GAMMA / BETA) * inv_gp3
+    drift = (1.0 / 3.0) * radius * ec_r
+    return kf, inv_kn, ec, drift, ec_z, minus, gp3, tfac, amp, amp_ec, phi_d * inv_phi, total
+
+
+PREPARED = 12
+
+
+def xc_derivs(prepared, s_own, s_mix, s_other):
+    kf, inv_kn, ec, drift, ec_z, minus, gp3, tfac, amp, amp_ec, phi_r, total = prepared
+    s2 = s_own * inv_kn * inv_kn
+    inv_den = 1.0 / (1.0 + (MU_X / KAPPA) * s2)
+    enh = (1.0 + KAPPA) - KAPPA * inv_den
+    enh_d = MU_X * inv_den * inv_den
+    dn_x = (-1.0 / math.pi) * kf * (enh - 2.0 * s2 * enh_d)
+    ds_x = (-3.0 / (8.0 * math.pi)) * enh_d * inv_kn
+    sigma = s_own + 2.0 * s_mix + s_other
+    t2 = sigma * tfac
     y = amp * t2
     den = 1.0 + y + y * y
     inv_d = 1.0 / den
     ct = (BETA / GAMMA) * t2
     q = ct * (1.0 + y) * inv_d
-    grad_h = GAMMA * phi3 * jnp.log(1.0 + q)
-    scale = GAMMA * phi3 / (1.0 + q) * inv_d * inv_d
+    grad_h = gp3 * jnp.log(1.0 + q)
+    scale = gp3 / (1.0 + q) * inv_d * inv_d
     h_t = scale * ((BETA / GAMMA) * (1.0 + 2.0 * y))
     h_a = -scale * (ct * t2) * (y * (2.0 + y))
-    h_ec = h_a * (amp * amp * ex * (GAMMA / BETA) * inv_gp3)
-    h_phi = inv_phi * (3.0 * (grad_h - ec * h_ec) - 2.0 * t2 * h_t)
+    h_ec = h_a * amp_ec
     one_ec = 1.0 + h_ec
-    e_n = ec + grad_h - (1.0 / 3.0) * radius * ec_r * one_ec - (7.0 / 3.0) * t2 * h_t
-    e_z = ec_z * one_ec + phi_d * h_phi
+    e_n = ec + grad_h - drift * one_ec - (7.0 / 3.0) * t2 * h_t
+    e_z = ec_z * one_ec + phi_r * (3.0 * (grad_h - ec * h_ec) - 2.0 * t2 * h_t)
     dn = dn_x + e_n + e_z * minus
     ds_c = total * h_t * tfac
     return dn, ds_x + ds_c, 2.0 * ds_c
@@ -125,7 +134,7 @@
 def kernel(
     orb_hbm, bands_hbm, core_hbm, out_ref,
     orb, dmat_ref, lane_ref, bands_ref, part, core, x_in, x_out, summed, z_in, zf_in, zf_sum, xf_in,
-    dens, grad, grad_o, flux, turned, x_line, x_res, x_back, y_line, y_res, y_back, base, final, x_fin, y_fin,
+    dens, dens_o, prepared, grad, grad_o, flux, turned, x_line, x_res, x_back, y_line, y_res, y_back, base, final, x_fin, y_fin,
     orb_sem, core_sem, bands_sem, hop_sem, xs_sem, xr_sem, zs_sem, zr_sem, fs_sem, fr_sem,
     ps_sem, pr_sem, ys_sem, yr_sem, gs_sem, gr_sem, bs_sem, br_sem,
 ):
@@ -426,9 +435,9 @@
 
     with jax.named_scope("fwd0"):
         pencils(dens, dens, 0)
-        send(dens, grad_o.at[3], ps_sem, pr_sem, partner)
+        send(dens, dens_o, ps_sem, pr_sem.at[0], partner)
         grad[2] = -along_lanes(dens[...])
-        send(grad.at[2], grad_o.at[2], ps_sem, pr_sem, partner)
+        send(grad.at[2], grad_o.at[2], ps_sem, pr_sem.at[1], partner)
     with jax.named_scope("drain0"):
         sent(part.at[0:3, 0:CH], xs_sem)
         sent(z_in, zs_sem)
@@ -444,19 +453,25 @@
     with jax.named_scope("x_lines0"):
         x_res[0] = along_rows(x_line[0])
         x_exchange(x_res.at[0], x_back, 1)
+    with jax.named_scope("prepare"):
+        arrived(dens_o, pr_sem.at[0])
+        step = 16
+        for i in range(0, N, step):
+            rows = slice(i, i + step)
+            for k, known in enumerate(xc_prepare(dens_o[rows, :], dens[rows, :])):
+                prepared[k, rows, :] = known
     with jax.named_scope("y_back0"):
         y_wait(y_back, 1)
-        send(y_back, grad_o.at[1], ps_sem, pr_sem, partner)
+        send(y_back, grad_o.at[1], ps_sem, pr_sem.at[1], partner)
     with jax.named_scope("x_back0"):
         x_wait(x_back, 1)
         for i in range(8):
             grad[0, 16 * i : 16 * i + 16, :] = x_back[pl.ds(i, 16, stride=8), :]
     with jax.named_scope("swap"):
-        send(grad.at[0], grad_o.at[0], ps_sem, pr_sem, partner)
-        arrived(grad_o, pr_sem)
+        send(grad.at[0], grad_o.at[0], ps_sem, pr_sem.at[1], partner)
+        arrived(grad_o, pr_sem.at[1])
 
     with jax.named_scope("xc"):
-        step = 16
         for i in range(0, N, step):
             rows = slice(i, i + step)
             o = (grad[0, rows, :], y_back[rows, :], grad[2, rows, :])
@@ -464,7 +479,8 @@
             s_own = g[0] * g[0] + g[1] * g[1] + g[2] * g[2]
             s_mix = g[0] * o[0] + g[1] * o[1] + g[2] * o[2]
             s_other = o[0] * o[0] + o[1] * o[1] + o[2] * o[2]
-            dn, ds, dm = xc_derivs(grad_o[3, rows, :], dens[rows, :], s_own, s_mix, s_other)
+            known = [prepared[k, rows, :] for k in range(PREPARED)]
+            dn, ds, dm = xc_derivs(known, s_own, s_mix, s_other)
             for a in range(3):
                 flux[a, rows, :] = 2.0 * ds * g[a] + dm * o[a]
             flux[3, rows, :] = dn
@@ -483,6 +499,7 @@
             sent(y_line.at[k], ys_sem.at[k])
             sent(x_line.at[k], gs_sem.at[k])
         sent(grad_o, ps_sem)
+        sent(dens_o, ps_sem)
     with jax.named_scope("y_wait1"):
         y_wait(y_line.at[1], 2)
     with jax.named_scope("y_lines1"):
@@ -533,8 +550,10 @@
             vm((NX4, 2, 16, N), F32),
             vm((NX4, 2, 16, N), F32),
             vm((N, N), F32),
+            vm((N, N), F32),
+            vm((PREPARED, N, N), F32),
             vm((3, N, N), F32),
-            vm((4, N, N), F32),
+            vm((3, N, N), F32),
             vm((4, N, N), F32),
             vm((2, N, N), F32),
             vm((2, N, N), F32),
@@ -558,7 +577,7 @@
             sem((2,)),
             sem((2,)),
             sem,
-            sem,
+            sem((2,)),
             sem((4,)),
             sem((4,)),
             sem((4,)),

time: 44.7 us -> 44.3 us (level)
    pallas_call x1, Pallas kernels: 44 us -> 43.6 us  [per_device(): pl.pallas_call(kernel, out_shape=jax.ShapeDtypeStruct((1, XR, YB, N), F32...]
where the time goes in v3:
time: 44.3 us; the launch traced here: 44.2 us
  Pallas kernels  43.6 us (98%)
  local copies, waits for them, and re-layouts  0.63 us (1%)
    pallas_call x1, Pallas kernels, per_device(): pl.pallas_call(kernel, out_shape=jax.ShapeDtypeStruct((1, XR, YB, N), F32...  43.6 us

profile of v3, /device:TPU:1, one launch (start us, length us, event | category | flops | bytes accessed | tf_op | source)
XLA Modules:
  0.0 44.2 jit_solution(4782619404945474736)
XLA Ops:
  0.0 43.6 %shard_map.37 = f32[1,16,8,128]{3,2,1,0:T(8,128)S(1)} custom-call(bf16[1,8,16,128,128]{4,3,2,1,0:T(8,128)(2,1)} %orb_hbm.1, s32[1,2]{1,0:T(1,128)} %bands_hbm.1, f32[16,128,128]{2,1,0:T(8,128)} %core_hbm.1), custom_call_target="tpu_custom_call" | custom-call | tf_op jit(solution)/shard_map/pallas_call | solution.py:533
  43.6 0.6 %copy.5 = f32[1,16,8,128]{3,2,1,0:T(8,128)} copy(f32[1,16,8,128]{3,2,1,0:T(8,128)S(1)} %shard_map.37) | data formatting | bytes 131072

commit v4 on v3

--- a/solution.py
+++ b/solution.py
@@ -134,7 +134,7 @@
 def kernel(
     orb_hbm, bands_hbm, core_hbm, out_ref,
     orb, dmat_ref, lane_ref, bands_ref, part, core, x_in, x_out, summed, z_in, zf_in, zf_sum, xf_in,
-    dens, dens_o, prepared, grad, grad_o, flux, turned, x_line, x_res, x_back, y_line, y_res, y_back, base, final, x_fin, y_fin,
+    dens, dens_o, prepared, grad, grad_o, flux, turned, x_line, x_line_n, x_res, x_res_n, x_back, y_line, y_line_n, y_res, y_res_n, y_back, base, final, x_fin, y_fin,
     orb_sem, core_sem, bands_sem, hop_sem, xs_sem, xr_sem, zs_sem, zr_sem, fs_sem, fr_sem,
     ps_sem, pr_sem, ys_sem, yr_sem, gs_sem, gr_sem, bs_sem, br_sem,
 ):
@@ -371,21 +371,24 @@
 
     holder = 1 - spin
 
-    def y_exchange(src, dst, k):
+    def pass_on(src, dst, send_sem, recv_sem, local):
+        if local:
+            dst[...] = src[...]
+        else:
+            send(src, dst, send_sem, recv_sem, partner)
+
+    def y_exchange(src, dst, ks, kr, core, local=False):
         for dx, dq in ((2, 1), (1, 1), (3, 1), (0, 1), (2, 0), (1, 0), (3, 0)):
             x, place = lax.rem(bx + dx, NX4), lax.rem(q + dq, 2)
             z = h + place * (3 - 2 * h)
             send(
                 src.at[rows_at(16 * (2 * x + place), 16), :], dst.at[rows_at(16 * member, 16), :],
-                ys_sem.at[k], yr_sem.at[k], (holder, x * NZ4 + z, grid),
+                ys_sem.at[ks], yr_sem.at[kr], (core, x * NZ4 + z, grid),
             )
         mine = rows_at(16 * member, 16)
-        send(src.at[mine, :], dst.at[mine, :], ys_sem.at[k], yr_sem.at[k], partner)
-
-    def y_wait(dst, k):
-        arrived(dst, yr_sem.at[k])
-
-    def x_exchange(src, dst, k):
+        pass_on(src.at[mine, :], dst.at[mine, :], ys_sem.at[ks], yr_sem.at[kr], local)
+
+    def x_exchange(src, dst, ks, kr, core, local=False, back=False):
         for de in (1, 0):
             for dz in (1, 0):
                 for dy in (2, 1, 3, 0):
@@ -395,19 +398,22 @@
                     g2 = lax.rem(gz + dz, 2) * GY + lax.rem(gy + dy, GY)
                     z = 2 * q + e2
                     there, here = 8 * e2 + g2, 2 * grid + h
-                    if k == 1:
+                    if back:
                         there, here = 2 * g2 + half_of(z), 8 * e + grid
                     send(
                         src.at[rows_at(8 * there, 8), :], dst.at[rows_at(8 * here, 8), :],
-                        gs_sem.at[k], gr_sem.at[k], (holder, bx * NZ4 + z, g2),
+                        gs_sem.at[ks], gr_sem.at[kr], (core, bx * NZ4 + z, g2),
                     )
         mine = (2 * grid + h, 8 * e + grid)
-        there, here = mine if k == 1 else mine[::-1]
+        there, here = mine if back else mine[::-1]
         there, here = rows_at(8 * there, 8), rows_at(8 * here, 8)
-        send(src.at[there, :], dst.at[here, :], gs_sem.at[k], gr_sem.at[k], partner)
-
-    def x_wait(dst, k):
-        arrived(dst, gr_sem.at[k])
+        pass_on(src.at[there, :], dst.at[here, :], gs_sem.at[ks], gr_sem.at[kr], local)
+
+    def y_wait(dst, k, local=False):
+        arrived(dst.at[0 : N - 16, :] if local else dst, yr_sem.at[k])
+
+    def x_wait(dst, k, local=False):
+        arrived(dst.at[0 : N - 8, :] if local else dst, gr_sem.at[k])
 
     def out_y():
         xr = 8 * h + member
@@ -427,14 +433,24 @@
                 gs_sem.at[3], gr_sem.at[3], (holder, band, g2),
             )
 
-    def pencils(y_src, x_src, k):
-        y_exchange(y_src, y_line.at[k], 2 * k)
+    def turn(src, dst):
         for t in range(16):
-            turned[k, 8 * t : 8 * t + 8, :] = x_src[pl.ds(t, 8, stride=16), :]
-        x_exchange(turned.at[k], x_line.at[k], 2 * k)
+            dst[8 * t : 8 * t + 8, :] = src[pl.ds(t, 8, stride=16), :]
 
     with jax.named_scope("fwd0"):
-        pencils(dens, dens, 0)
+
+        @pl.when(spin == 0)
+        def _():
+            y_exchange(dens, y_line.at[0], 0, 0, 1)
+            turn(dens, turned.at[0])
+            x_exchange(turned.at[0], x_line.at[0], 0, 0, 1)
+
+        @pl.when(spin == 1)
+        def _():
+            y_exchange(dens, y_line_n, 4, 4, 1, local=True)
+            turn(dens, turned.at[0])
+            x_exchange(turned.at[0], x_line_n, 4, 4, 1, local=True)
+
         send(dens, dens_o, ps_sem, pr_sem.at[0], partner)
         grad[2] = -along_lanes(dens[...])
         send(grad.at[2], grad_o.at[2], ps_sem, pr_sem.at[1], partner)
@@ -443,16 +459,6 @@
         sent(z_in, zs_sem)
         sent(zf_in, fs_sem.at[0])
         sent(xf_in, fs_sem.at[1])
-    with jax.named_scope("y_wait0"):
-        y_wait(y_line.at[0], 0)
-    with jax.named_scope("y_lines0"):
-        y_res[0] = along_rows(y_line[0])
-        y_exchange(y_res.at[0], y_back, 1)
-    with jax.named_scope("x_wait0"):
-        x_wait(x_line.at[0], 0)
-    with jax.named_scope("x_lines0"):
-        x_res[0] = along_rows(x_line[0])
-        x_exchange(x_res.at[0], x_back, 1)
     with jax.named_scope("prepare"):
         arrived(dens_o, pr_sem.at[0])
         step = 16
@@ -460,11 +466,30 @@
             rows = slice(i, i + step)
             for k, known in enumerate(xc_prepare(dens_o[rows, :], dens[rows, :])):
                 prepared[k, rows, :] = known
+    with jax.named_scope("lines0"):
+
+        @pl.when(spin == 1)
+        def _():
+            y_wait(y_line.at[0], 0)
+            y_res[0] = along_rows(y_line[0])
+            y_exchange(y_res.at[0], y_back, 1, 1, 0)
+            x_wait(x_line.at[0], 0)
+            x_res[0] = along_rows(x_line[0])
+            x_exchange(x_res.at[0], x_back, 1, 1, 0, back=True)
+            y_wait(y_line_n, 4, local=True)
+            y_res_n[...] = along_rows(y_line_n[...])
+            y_exchange(y_res_n, y_back, 1, 1, 1, local=True)
+            x_wait(x_line_n, 4, local=True)
+            x_res_n[...] = along_rows(x_line_n[...])
+            x_exchange(x_res_n, x_back, 1, 1, 1, local=True, back=True)
+
     with jax.named_scope("y_back0"):
-        y_wait(y_back, 1)
+        pl.when(spin == 0)(lambda: y_wait(y_back, 1))
+        pl.when(spin == 1)(lambda: y_wait(y_back, 1, local=True))
         send(y_back, grad_o.at[1], ps_sem, pr_sem.at[1], partner)
     with jax.named_scope("x_back0"):
-        x_wait(x_back, 1)
+        pl.when(spin == 0)(lambda: x_wait(x_back, 1))
+        pl.when(spin == 1)(lambda: x_wait(x_back, 1, local=True))
         for i in range(8):
             grad[0, 16 * i : 16 * i + 16, :] = x_back[pl.ds(i, 16, stride=8), :]
     with jax.named_scope("swap"):
@@ -486,7 +511,9 @@
             flux[3, rows, :] = dn
 
     with jax.named_scope("fwd1"):
-        pencils(flux.at[1], flux.at[0], 1)
+        y_exchange(flux.at[1], y_line.at[1], 2, 2, holder)
+        turn(flux.at[0], turned.at[1])
+        x_exchange(turned.at[1], x_line.at[1], 2, 2, holder)
         base[...] = (flux[3] + along_lanes(flux[2])).reshape(8, 16, N)
         there = lax.rem(e + 1, 2)
         send(
@@ -495,9 +522,20 @@
         )
         final[h] = base[:, rows_at(8 * e, 8), :]
     with jax.named_scope("drain1"):
-        for k in (0, 1):
-            sent(y_line.at[k], ys_sem.at[k])
-            sent(x_line.at[k], gs_sem.at[k])
+
+        @pl.when(spin == 0)
+        def _():
+            sent(y_line.at[0], ys_sem.at[0])
+            sent(x_line.at[0], gs_sem.at[0])
+
+        @pl.when(spin == 1)
+        def _():
+            for k in (1, 4):
+                sent(y_line.at[0, 0 : N - 16, :], ys_sem.at[k])
+                sent(x_line.at[0, 0 : N - 8, :], gs_sem.at[k])
+            sent(y_line.at[0], ys_sem.at[1])
+            sent(x_line.at[0], gs_sem.at[1])
+
         sent(grad_o, ps_sem)
         sent(dens_o, ps_sem)
     with jax.named_scope("y_wait1"):
@@ -557,10 +595,14 @@
             vm((4, N, N), F32),
             vm((2, N, N), F32),
             vm((2, N, N), F32),
+            vm((N, N), F32),
             vm((2, N, N), F32),
             vm((N, N), F32),
+            vm((N, N), F32),
             vm((2, N, N), F32),
+            vm((N, N), F32),
             vm((2, N, N), F32),
+            vm((N, N), F32),
             vm((N, N), F32),
             vm((8, 16, N), F32),
             vm((2, 8, YB, N), F32),
@@ -578,10 +620,10 @@
             sem((2,)),
             sem,
             sem((2,)),
-            sem((4,)),
-            sem((4,)),
-            sem((4,)),
-            sem((4,)),
+            sem((5,)),
+            sem((5,)),
+            sem((5,)),
+            sem((5,)),
             sem,
             sem,
         ],

time: 44.3 us -> 44.3 us (level)
  no operation moved by 1% of the time
where the time goes in v4:
time: 44.3 us
  Pallas kernels  43.6 us (98%)
  local copies, waits for them, and re-layouts  0.63 us (1%)
    pallas_call x1, Pallas kernels, per_device(): pl.pallas_call(kernel, out_shape=jax.ShapeDtypeStruct((1, XR, YB, N), F32...  43.6 us

profile of v4, /device:TPU:1, one launch (start us, length us, event | category | flops | bytes accessed | tf_op | source)
XLA Modules:
  0.0 44.3 jit_solution(1885027725123169132)
XLA Ops:
  0.0 43.6 %shard_map.37 = f32[1,16,8,128]{3,2,1,0:T(8,128)S(1)} custom-call(bf16[1,8,16,128,128]{4,3,2,1,0:T(8,128)(2,1)} %orb_hbm.1, s32[1,2]{1,0:T(1,128)} %bands_hbm.1, f32[16,128,128]{2,1,0:T(8,128)} %core_hbm.1), custom_call_target="tpu_custom_call" | custom-call | tf_op jit(solution)/shard_map/pallas_call | solution.py:571
  43.6 0.6 %copy.5 = f32[1,16,8,128]{3,2,1,0:T(8,128)} copy(f32[1,16,8,128]{3,2,1,0:T(8,128)S(1)} %shard_map.37) | data formatting | bytes 131072

commit v5 on v4

--- a/solution.py
+++ b/solution.py
@@ -369,8 +369,6 @@
         hi, lo = halves(x)
         return jnp.dot(jnp.concatenate([hi, hi, lo], 1), lane_ref[...], preferred_element_type=F32)
 
-    holder = 1 - spin
-
     def pass_on(src, dst, send_sem, recv_sem, local):
         if local:
             dst[...] = src[...]
@@ -415,23 +413,27 @@
     def x_wait(dst, k, local=False):
         arrived(dst.at[0 : N - 8, :] if local else dst, gr_sem.at[k])
 
-    def out_y():
-        xr = 8 * h + member
+    def out_y(src, core, local=False):
+        xr = rows_at(8 * (8 * h + member), 8)
         for dx in (2, 1, 3, 0):
             for dz in (2, 1, 3, 0):
-                b2 = lax.rem(bx + dx, NX4) * NZ4 + lax.rem(bz + dz, NZ4)
-                send(
-                    y_res.at[1, rows_at(8 * b2, 8), :], y_fin.at[rows_at(8 * xr, 8), :],
-                    ys_sem.at[3], yr_sem.at[3], (holder, b2, grid),
-                )
-
-    def out_x():
-        for dz, dy in ((1, 2), (1, 1), (1, 3), (0, 2), (1, 0), (0, 1), (0, 3), (0, 0)):
+                if (dx, dz) != (0, 0):
+                    b2 = lax.rem(bx + dx, NX4) * NZ4 + lax.rem(bz + dz, NZ4)
+                    send(
+                        src.at[rows_at(8 * b2, 8), :], y_fin.at[xr, :],
+                        ys_sem.at[3], yr_sem.at[3], (core, b2, grid),
+                    )
+        pass_on(src.at[rows_at(8 * band, 8), :], y_fin.at[xr, :], ys_sem.at[3], yr_sem.at[3], local)
+
+    def out_x(src, core, local=False):
+        mine = rows_at(XR * grid, XR)
+        for dz, dy in ((1, 2), (1, 1), (1, 3), (0, 2), (1, 0), (0, 1), (0, 3)):
             g2 = lax.rem(gz + dz, 2) * GY + lax.rem(gy + dy, GY)
             send(
-                x_res.at[1, rows_at(XR * g2, XR), :], x_fin.at[rows_at(XR * grid, XR), :],
-                gs_sem.at[3], gr_sem.at[3], (holder, band, g2),
+                src.at[rows_at(XR * g2, XR), :], x_fin.at[mine, :],
+                gs_sem.at[3], gr_sem.at[3], (core, band, g2),
             )
+        pass_on(src.at[mine, :], x_fin.at[mine, :], gs_sem.at[3], gr_sem.at[3], local)
 
     def turn(src, dst):
         for t in range(16):
@@ -447,9 +449,9 @@
 
         @pl.when(spin == 1)
         def _():
-            y_exchange(dens, y_line_n, 4, 4, 1, local=True)
+            y_exchange(dens, y_line_n.at[0], 4, 4, 1, local=True)
             turn(dens, turned.at[0])
-            x_exchange(turned.at[0], x_line_n, 4, 4, 1, local=True)
+            x_exchange(turned.at[0], x_line_n.at[0], 4, 4, 1, local=True)
 
         send(dens, dens_o, ps_sem, pr_sem.at[0], partner)
         grad[2] = -along_lanes(dens[...])
@@ -476,12 +478,12 @@
             x_wait(x_line.at[0], 0)
             x_res[0] = along_rows(x_line[0])
             x_exchange(x_res.at[0], x_back, 1, 1, 0, back=True)
-            y_wait(y_line_n, 4, local=True)
-            y_res_n[...] = along_rows(y_line_n[...])
-            y_exchange(y_res_n, y_back, 1, 1, 1, local=True)
-            x_wait(x_line_n, 4, local=True)
-            x_res_n[...] = along_rows(x_line_n[...])
-            x_exchange(x_res_n, x_back, 1, 1, 1, local=True, back=True)
+            y_wait(y_line_n.at[0], 4, local=True)
+            y_res_n[0] = along_rows(y_line_n[0])
+            y_exchange(y_res_n.at[0], y_back, 1, 1, 1, local=True)
+            x_wait(x_line_n.at[0], 4, local=True)
+            x_res_n[0] = along_rows(x_line_n[0])
+            x_exchange(x_res_n.at[0], x_back, 1, 1, 1, local=True, back=True)
 
     with jax.named_scope("y_back0"):
         pl.when(spin == 0)(lambda: y_wait(y_back, 1))
@@ -511,9 +513,19 @@
             flux[3, rows, :] = dn
 
     with jax.named_scope("fwd1"):
-        y_exchange(flux.at[1], y_line.at[1], 2, 2, holder)
-        turn(flux.at[0], turned.at[1])
-        x_exchange(turned.at[1], x_line.at[1], 2, 2, holder)
+
+        @pl.when(spin == 0)
+        def _():
+            y_exchange(flux.at[1], y_line.at[1], 2, 2, 1)
+            turn(flux.at[0], turned.at[1])
+            x_exchange(turned.at[1], x_line.at[1], 2, 2, 1)
+
+        @pl.when(spin == 1)
+        def _():
+            y_exchange(flux.at[1], y_line_n.at[1], 5, 5, 1, local=True)
+            turn(flux.at[0], turned.at[1])
+            x_exchange(turned.at[1], x_line_n.at[1], 5, 5, 1, local=True)
+
         base[...] = (flux[3] + along_lanes(flux[2])).reshape(8, 16, N)
         there = lax.rem(e + 1, 2)
         send(
@@ -538,28 +550,49 @@
 
         sent(grad_o, ps_sem)
         sent(dens_o, ps_sem)
-    with jax.named_scope("y_wait1"):
-        y_wait(y_line.at[1], 2)
-    with jax.named_scope("y_lines1"):
-        y_res[1] = along_rows(y_line[1])
-        out_y()
-    with jax.named_scope("x_wait1"):
-        x_wait(x_line.at[1], 2)
-    with jax.named_scope("x_lines1"):
-        x_res[1] = along_rows(x_line[1])
-        out_x()
+    with jax.named_scope("lines1"):
+
+        @pl.when(spin == 1)
+        def _():
+            y_wait(y_line_n.at[1], 5, local=True)
+            y_res_n[1] = along_rows(y_line_n[1])
+            out_y(y_res_n.at[1], 1, local=True)
+            x_wait(x_line_n.at[1], 5, local=True)
+            x_res_n[1] = along_rows(x_line_n[1])
+            out_x(x_res_n.at[1], 1, local=True)
+            y_wait(y_line.at[1], 2)
+            y_res[1] = along_rows(y_line[1])
+            out_y(y_res.at[1], 0)
+            x_wait(x_line.at[1], 2)
+            x_res[1] = along_rows(x_line[1])
+            out_x(x_res.at[1], 0)
+
     with jax.named_scope("drain2"):
-        for k in (2, 3):
-            sent(y_line.at[0], ys_sem.at[k])
-            sent(x_line.at[0], gs_sem.at[k])
+
+        @pl.when(spin == 0)
+        def _():
+            sent(y_line.at[0], ys_sem.at[2])
+            sent(x_line.at[0], gs_sem.at[2])
+
+        @pl.when(spin == 1)
+        def _():
+            sent(y_line.at[0, 0 : N - 16, :], ys_sem.at[5])
+            sent(x_line.at[0, 0 : N - 8, :], gs_sem.at[5])
+            sent(y_line.at[0, 0 : N - YB, :], ys_sem.at[3])
+            sent(x_line.at[0, 0 : N - XR, :], gs_sem.at[3])
+            sent(y_line.at[0], ys_sem.at[3])
+            sent(x_line.at[0], gs_sem.at[3])
+
         sent(final.at[0], bs_sem)
         arrived(final.at[0], br_sem)
     with jax.named_scope("x_back1"):
-        arrived(x_fin, gr_sem.at[3])
+        pl.when(spin == 0)(lambda: arrived(x_fin, gr_sem.at[3]))
+        pl.when(spin == 1)(lambda: arrived(x_fin.at[0 : N - XR, :], gr_sem.at[3]))
         for i in range(XR):
             out_ref[0, i] = final[i // 8, i % 8] - x_fin[pl.ds(i, YB, stride=XR), :]
     with jax.named_scope("y_back1"):
-        arrived(y_fin, yr_sem.at[3])
+        pl.when(spin == 0)(lambda: arrived(y_fin, yr_sem.at[3]))
+        pl.when(spin == 1)(lambda: arrived(y_fin.at[0 : N - YB, :], yr_sem.at[3]))
     with jax.named_scope("tail"):
         out_ref[0] = out_ref[0] - y_fin[...].reshape(XR, YB, N)
 
@@ -595,14 +628,14 @@
             vm((4, N, N), F32),
             vm((2, N, N), F32),
             vm((2, N, N), F32),
+            vm((2, N, N), F32),
+            vm((2, N, N), F32),
+            vm((2, N, N), F32),
             vm((N, N), F32),
             vm((2, N, N), F32),
-            vm((N, N), F32),
-            vm((N, N), F32),
-            vm((2, N, N), F32),
-            vm((N, N), F32),
-            vm((2, N, N), F32),
-            vm((N, N), F32),
+            vm((2, N, N), F32),
+            vm((2, N, N), F32),
+            vm((2, N, N), F32),
             vm((N, N), F32),
             vm((8, 16, N), F32),
             vm((2, 8, YB, N), F32),
@@ -620,10 +653,10 @@
             sem((2,)),
             sem,
             sem((2,)),
-            sem((5,)),
-            sem((5,)),
-            sem((5,)),
-            sem((5,)),
+            sem((6,)),
+            sem((6,)),
+            sem((6,)),
+            sem((6,)),
             sem,
             sem,
         ],

time: 44.3 us -> 43.2 us (0.975)
  Pallas kernels: 43.6 us -> 42.5 us
    pallas_call x1, Pallas kernels: 43.6 us -> 42.5 us  [per_device(): pl.pallas_call(kernel, out_shape=jax.ShapeDtypeStruct((1, XR, YB, N), F32...]
where the time goes in v5:
time: 43.2 us
  Pallas kernels  42.5 us (98%)
  local copies, waits for them, and re-layouts  0.63 us (1%)
    pallas_call x1, Pallas kernels, per_device(): pl.pallas_call(kernel, out_shape=jax.ShapeDtypeStruct((1, XR, YB, N), F32...  42.5 us

profile of v5, /device:TPU:1, one launch (start us, length us, event | category | flops | bytes accessed | tf_op | source)
XLA Modules:
  0.0 43.2 jit_solution(11153037309048034448)
XLA Ops:
  0.0 42.5 %shard_map.37 = f32[1,16,8,128]{3,2,1,0:T(8,128)S(1)} custom-call(bf16[1,8,16,128,128]{4,3,2,1,0:T(8,128)(2,1)} %orb_hbm.1, s32[1,2]{1,0:T(1,128)} %bands_hbm.1, f32[16,128,128]{2,1,0:T(8,128)} %core_hbm.1), custom_call_target="tpu_custom_call" | custom-call | tf_op jit(solution)/shard_map/pallas_call | solution.py:604
  42.5 0.6 %copy.5 = f32[1,16,8,128]{3,2,1,0:T(8,128)} copy(f32[1,16,8,128]{3,2,1,0:T(8,128)S(1)} %shard_map.37) | data formatting | bytes 131072

commit v6 on v5

--- a/solution.py
+++ b/solution.py
@@ -136,7 +136,7 @@
     orb, dmat_ref, lane_ref, bands_ref, part, core, x_in, x_out, summed, z_in, zf_in, zf_sum, xf_in,
     dens, dens_o, prepared, grad, grad_o, flux, turned, x_line, x_line_n, x_res, x_res_n, x_back, y_line, y_line_n, y_res, y_res_n, y_back, base, final, x_fin, y_fin,
     orb_sem, core_sem, bands_sem, hop_sem, xs_sem, xr_sem, zs_sem, zr_sem, fs_sem, fr_sem,
-    ps_sem, pr_sem, ys_sem, yr_sem, gs_sem, gr_sem, bs_sem, br_sem,
+    ps_sem, pr_sem, es_sem, yr_sem, gr_sem, bs_sem, br_sem,
 ):
     spin = lax.axis_index("spin")
     band = lax.axis_index("band")
@@ -381,10 +381,10 @@
             z = h + place * (3 - 2 * h)
             send(
                 src.at[rows_at(16 * (2 * x + place), 16), :], dst.at[rows_at(16 * member, 16), :],
-                ys_sem.at[ks], yr_sem.at[kr], (core, x * NZ4 + z, grid),
+                es_sem, yr_sem.at[kr], (core, x * NZ4 + z, grid),
             )
         mine = rows_at(16 * member, 16)
-        pass_on(src.at[mine, :], dst.at[mine, :], ys_sem.at[ks], yr_sem.at[kr], local)
+        pass_on(src.at[mine, :], dst.at[mine, :], es_sem, yr_sem.at[kr], local)
 
     def x_exchange(src, dst, ks, kr, core, local=False, back=False):
         for de in (1, 0):
@@ -400,12 +400,12 @@
                         there, here = 2 * g2 + half_of(z), 8 * e + grid
                     send(
                         src.at[rows_at(8 * there, 8), :], dst.at[rows_at(8 * here, 8), :],
-                        gs_sem.at[ks], gr_sem.at[kr], (core, bx * NZ4 + z, g2),
+                        es_sem, gr_sem.at[kr], (core, bx * NZ4 + z, g2),
                     )
         mine = (2 * grid + h, 8 * e + grid)
         there, here = mine if back else mine[::-1]
         there, here = rows_at(8 * there, 8), rows_at(8 * here, 8)
-        pass_on(src.at[there, :], dst.at[here, :], gs_sem.at[ks], gr_sem.at[kr], local)
+        pass_on(src.at[there, :], dst.at[here, :], es_sem, gr_sem.at[kr], local)
 
     def y_wait(dst, k, local=False):
         arrived(dst.at[0 : N - 16, :] if local else dst, yr_sem.at[k])
@@ -421,9 +421,9 @@
                     b2 = lax.rem(bx + dx, NX4) * NZ4 + lax.rem(bz + dz, NZ4)
                     send(
                         src.at[rows_at(8 * b2, 8), :], y_fin.at[xr, :],
-                        ys_sem.at[3], yr_sem.at[3], (core, b2, grid),
+                        es_sem, yr_sem.at[3], (core, b2, grid),
                     )
-        pass_on(src.at[rows_at(8 * band, 8), :], y_fin.at[xr, :], ys_sem.at[3], yr_sem.at[3], local)
+        pass_on(src.at[rows_at(8 * band, 8), :], y_fin.at[xr, :], es_sem, yr_sem.at[3], local)
 
     def out_x(src, core, local=False):
         mine = rows_at(XR * grid, XR)
@@ -431,9 +431,9 @@
             g2 = lax.rem(gz + dz, 2) * GY + lax.rem(gy + dy, GY)
             send(
                 src.at[rows_at(XR * g2, XR), :], x_fin.at[mine, :],
-                gs_sem.at[3], gr_sem.at[3], (core, band, g2),
+                es_sem, gr_sem.at[3], (core, band, g2),
             )
-        pass_on(src.at[mine, :], x_fin.at[mine, :], gs_sem.at[3], gr_sem.at[3], local)
+        pass_on(src.at[mine, :], x_fin.at[mine, :], es_sem, gr_sem.at[3], local)
 
     def turn(src, dst):
         for t in range(16):
@@ -534,20 +534,6 @@
         )
         final[h] = base[:, rows_at(8 * e, 8), :]
     with jax.named_scope("drain1"):
-
-        @pl.when(spin == 0)
-        def _():
-            sent(y_line.at[0], ys_sem.at[0])
-            sent(x_line.at[0], gs_sem.at[0])
-
-        @pl.when(spin == 1)
-        def _():
-            for k in (1, 4):
-                sent(y_line.at[0, 0 : N - 16, :], ys_sem.at[k])
-                sent(x_line.at[0, 0 : N - 8, :], gs_sem.at[k])
-            sent(y_line.at[0], ys_sem.at[1])
-            sent(x_line.at[0], gs_sem.at[1])
-
         sent(grad_o, ps_sem)
         sent(dens_o, ps_sem)
     with jax.named_scope("lines1"):
@@ -571,17 +557,15 @@
 
         @pl.when(spin == 0)
         def _():
-            sent(y_line.at[0], ys_sem.at[2])
-            sent(x_line.at[0], gs_sem.at[2])
+            for _ in range(2):
+                sent(y_line, es_sem)
 
         @pl.when(spin == 1)
         def _():
-            sent(y_line.at[0, 0 : N - 16, :], ys_sem.at[5])
-            sent(x_line.at[0, 0 : N - 8, :], gs_sem.at[5])
-            sent(y_line.at[0, 0 : N - YB, :], ys_sem.at[3])
-            sent(x_line.at[0, 0 : N - XR, :], gs_sem.at[3])
-            sent(y_line.at[0], ys_sem.at[3])
-            sent(x_line.at[0], gs_sem.at[3])
+            for _ in range(2):
+                sent(y_line, es_sem)
+            for kept in (16, 16, 16, 8, 8, 8, YB, XR):
+                sent(y_line.at[0, 0 : N - kept, :], es_sem)
 
         sent(final.at[0], bs_sem)
         arrived(final.at[0], br_sem)
@@ -653,8 +637,7 @@
             sem((2,)),
             sem,
             sem((2,)),
-            sem((6,)),
-            sem((6,)),
+            sem,
             sem((6,)),
             sem((6,)),
             sem,

time: 43.2 us -> 43.1 us (level)
  no operation moved by 1% of the time
where the time goes in v6:
time: 43.1 us
  Pallas kernels  42.4 us (98%)
  local copies, waits for them, and re-layouts  0.63 us (1%)
    pallas_call x1, Pallas kernels, per_device(): pl.pallas_call(kernel, out_shape=jax.ShapeDtypeStruct((1, XR, YB, N), F32...  42.4 us

profile of v6, /device:TPU:1, one launch (start us, length us, event | category | flops | bytes accessed | tf_op | source)
XLA Modules:
  0.0 43.1 jit_solution(12528092074126595863)
XLA Ops:
  0.0 42.4 %shard_map.37 = f32[1,16,8,128]{3,2,1,0:T(8,128)S(1)} custom-call(bf16[1,8,16,128,128]{4,3,2,1,0:T(8,128)(2,1)} %orb_hbm.1, s32[1,2]{1,0:T(1,128)} %bands_hbm.1, f32[16,128,128]{2,1,0:T(8,128)} %core_hbm.1), custom_call_target="tpu_custom_call" | custom-call | tf_op jit(solution)/shard_map/pallas_call | solution.py:588
  42.4 0.6 %copy.5 = f32[1,16,8,128]{3,2,1,0:T(8,128)} copy(f32[1,16,8,128]{3,2,1,0:T(8,128)S(1)} %shard_map.37) | data formatting | bytes 131072

commit v7 on v5

--- a/solution.py
+++ b/solution.py
@@ -498,6 +498,19 @@
         send(grad.at[0], grad_o.at[0], ps_sem, pr_sem.at[1], partner)
         arrived(grad_o, pr_sem.at[1])
 
+    def flux_row(m):
+        z = h if m % 2 == 0 else 3 - h
+        src, mine = flux.at[1, 16 * m : 16 * m + 16, :], rows_at(16 * member, 16)
+        device = (1, m // 2 * NZ4 + z, grid)
+
+        @pl.when(spin == 0)
+        def _():
+            send(src, y_line.at[1, mine, :], ys_sem.at[2], yr_sem.at[2], device)
+
+        @pl.when((spin == 1) & (member != m))
+        def _():
+            send(src, y_line_n.at[1, mine, :], ys_sem.at[5], yr_sem.at[5], device)
+
     with jax.named_scope("xc"):
         for i in range(0, N, step):
             rows = slice(i, i + step)
@@ -511,18 +524,21 @@
             for a in range(3):
                 flux[a, rows, :] = 2.0 * ds * g[a] + dm * o[a]
             flux[3, rows, :] = dn
+            if i % 64 == 48:
+                for m in range(i // 16 - 3, i // 16 + 1):
+                    flux_row(m)
 
     with jax.named_scope("fwd1"):
 
         @pl.when(spin == 0)
         def _():
-            y_exchange(flux.at[1], y_line.at[1], 2, 2, 1)
             turn(flux.at[0], turned.at[1])
             x_exchange(turned.at[1], x_line.at[1], 2, 2, 1)
 
         @pl.when(spin == 1)
         def _():
-            y_exchange(flux.at[1], y_line_n.at[1], 5, 5, 1, local=True)
+            mine = rows_at(16 * member, 16)
+            y_line_n[1, mine, :] = flux[1, mine, :]
             turn(flux.at[0], turned.at[1])
             x_exchange(turned.at[1], x_line_n.at[1], 5, 5, 1, local=True)
 

time: 43.2 us -> 43.3 us (level)
  no operation moved by 1% of the time
where the time goes in v7:
time: 43.3 us; the launch traced here: 43.2 us
  Pallas kernels  42.6 us (98%)
  local copies, waits for them, and re-layouts  0.63 us (1%)
    pallas_call x1, Pallas kernels, per_device(): pl.pallas_call(kernel, out_shape=jax.ShapeDtypeStruct((1, XR, YB, N), F32...  42.6 us

profile of v7, /device:TPU:1, one launch (start us, length us, event | category | flops | bytes accessed | tf_op | source)
XLA Modules:
  0.0 43.2 jit_solution(3448142461282980982)
XLA Ops:
  0.0 42.6 %shard_map.37 = f32[1,16,8,128]{3,2,1,0:T(8,128)S(1)} custom-call(bf16[1,8,16,128,128]{4,3,2,1,0:T(8,128)(2,1)} %orb_hbm.1, s32[1,2]{1,0:T(1,128)} %bands_hbm.1, f32[16,128,128]{2,1,0:T(8,128)} %core_hbm.1), custom_call_target="tpu_custom_call" | custom-call | tf_op jit(solution)/shard_map/pallas_call | solution.py:620
  42.6 0.6 %copy.5 = f32[1,16,8,128]{3,2,1,0:T(8,128)} copy(f32[1,16,8,128]{3,2,1,0:T(8,128)S(1)} %shard_map.37) | data formatting | bytes 131072
